TPU v7x, 128 devices: a whole 4x4x4 slice. The times are simulated.
128 devices in a mesh: gx: 8 (over y_hi, z), gy: 4 (over x), gz: 4 (over y_lo, core).
Axes of the slice: x: 4, y: 4 (y_hi: 2, y_lo: 2; y = y_hi * 2 + y_lo), z: 4, core: 2. Of those that a mesh axis runs over, the one named last changes fastest.
Arguments:
- density: float32 [128, 64, 512], P('gx', 'gy', 'gz'), may hold values from 0.005 to 0.6, as said below
- coupling: float32 [14, 14], replicated, may hold values from -0.3 to 1.5, as said below
Outputs:
- potentials: float32 [14, 128, 64, 512], P(None, 'gx', 'gy', 'gz')
Inputs may be any that keep to these rules, and one draw needn't show every extreme that they name: Positive density. `coupling`: symmetric.
All inputs are finite; a program needn't handle non-finite values.
Results may differ from a plain program's by a relative error of at most 0.0003.
Values sent between devices are 32-bit elements; how exact they have to be, the bound alone decides.
A program may use at most 128 MiB of HBM per device.

v0:
```python
import functools
import math

import jax
import jax.numpy as jnp
import numpy as np
from jax import lax
from jax.experimental import pallas as pl
from jax.experimental.pallas import tpu as pltpu
from jax.sharding import PartitionSpec as P

MESH = pl.DeviceIdType.MESH
F32 = jnp.float32
BF16 = jnp.bfloat16

NQ = 14
NX, NY, NZ = 128, 64, 512
CHUNKS = 2
QC = NQ // CHUNKS
KNOTS = NQ + 2
COLS = NY * NZ // NX
SUMS = 2 * NQ - 1

ZAB = 0.8491 / 9.0
Q_CUT = 5.0
STEP = 0.07
LOCAL = 0.25
LAM = math.sqrt(3.0) - 2.0


def frequencies(length):
    half = length // 2
    return np.array(list(range(half + 1)) + list(range(1, half)), dtype=np.float64)


def basis(length):
    half = length // 2
    points = np.arange(length)[:, None]
    waves = frequencies(length)[None, :]
    angle = 2.0 * np.pi / length * np.mod(points * waves, length)
    table = np.where(np.arange(length)[None, :] <= half, np.cos(angle), np.sin(angle))
    scale = np.full((1, length), math.sqrt(2.0 / length))
    scale[0, 0] = scale[0, half] = math.sqrt(1.0 / length)
    return table * scale


def halves(table):
    high = table.astype(BF16)
    low = (table - high.astype(np.float64)).astype(BF16)
    return high, low


def left_table(table):
    high, low = halves(table)
    return np.concatenate([high, high, low], axis=1)


def wave_squared(length):
    return (2.0 * np.pi / length * frequencies(length)) ** 2


def split(value):
    high = value.astype(BF16)
    return high, (value - high.astype(F32)).astype(BF16)


def left_multiply(table, value):
    high, low = split(value)
    return jnp.dot(table, jnp.concatenate([high, low, high], axis=0), preferred_element_type=F32)


def right_multiply(value, table_ref, transposed):
    high, low = split(value)
    rows = jnp.concatenate([high, low, high], axis=1)
    side = 1 if transposed else 0
    weights = jnp.concatenate([table_ref[0], table_ref[0], table_ref[1]], axis=side)
    return lax.dot_general(rows, weights, (((1,), (side,)), ((), ())), preferred_element_type=F32)


def kernel(
    sizes, dens, coup, tz, ty_f, ty_i, tx_f, tx_i, fx2, fz2, out,
    planes, q_buf, top_src, tops, thetas, mid, send1, recv1, spec, gain, prod, send2, recv2, send3,
    ssem, rsem,
):
    devices = NX
    nx, ny, nz = sizes
    group = ny * nz
    ix, iy, iz = lax.axis_index("gx"), lax.axis_index("gy"), lax.axis_index("gz")
    me = (ix * ny + iy) * nz + iz
    block_x, block_y, block_z = NX // nx, NY // ny, NZ // nz
    per_row = NZ // COLS

    def ids(p):
        return {"gx": p // group, "gy": (p // nz) % ny, "gz": p % nz}

    def send(src, dst, slot, p):
        pltpu.make_async_remote_copy(
            src, dst, ssem.at[slot], rsem.at[slot], device_id=ids(p), device_id_type=MESH
        ).start()

    def keep(src, dst, slot):
        pltpu.make_async_copy(src, dst, rsem.at[slot]).start()

    def received(ref, slot):
        pltpu.make_async_copy(ref, ref, rsem.at[slot]).wait()

    def sent(rows, slot):
        full, rest = divmod(rows, NX)
        if full:
            part = recv1.at[pl.ds(0, full)]
            pltpu.make_async_copy(part, part, ssem.at[slot]).wait()
        if rest // 8:
            part = recv1.at[0, pl.ds(0, rest // 8 * 8)]
            pltpu.make_async_copy(part, part, ssem.at[slot]).wait()
        for _ in range(rest % 8):
            part = recv1.at[0, 0]
            pltpu.make_async_copy(part, part, ssem.at[slot]).wait()

    barrier = pltpu.get_barrier_semaphore()

    def greet(d, carry):
        p = (me + d) % devices
        pl.semaphore_signal(barrier, inc=1, device_id=ids(p), device_id_type=MESH)
        return carry

    lax.fori_loop(1, devices, greet, 0)
    pl.semaphore_wait(barrier, devices - 1)

    here_y = pl.ds(pl.multiple_of(iy * block_y, 8), block_y)
    here_z = pl.ds(pl.multiple_of(iz * block_z, 128), block_z)
    for shift in range(5):

        def give(r, carry, shift=shift):
            row = (me + r * 5 + shift) % block_x
            p = (ix * block_x + row - (shift - 2) + devices) % devices
            src, dst = dens.at[row], planes.at[shift, here_y, here_z]

            @pl.when(p != me)
            def _():
                send(src, dst, 0, p)

            @pl.when(p == me)
            def _():
                keep(src, dst, 0)

            return carry

        lax.fori_loop(0, block_x, give, 0)
    received(planes, 0)

    own = planes[2]
    slope_x = (8.0 * (planes[3] - planes[1]) - (planes[4] - planes[0])) / 12.0
    grad_sq = slope_x * slope_x
    for axis, length in ((0, NY), (1, NZ)):
        nearer = pltpu.roll(own, length - 1, axis) - pltpu.roll(own, 1, axis)
        farther = pltpu.roll(own, length - 2, axis) - pltpu.roll(own, 2, axis)
        slope = (8.0 * nearer - farther) / 12.0
        grad_sq = grad_sq + slope * slope
    cube = (3.0 * math.pi * math.pi) * own
    fermi_k = jnp.exp(jnp.log(cube) / 3.0)
    fermi_k = fermi_k - (fermi_k - cube / (fermi_k * fermi_k)) * (1.0 / 3.0)
    reduced = grad_sq / (4.0 * fermi_k * fermi_k * own * own)
    scaled = fermi_k * (1.0 + ZAB * reduced) / Q_CUT
    series = jnp.full_like(scaled, 1.0 / 12.0)
    for order in range(11, 0, -1):
        series = series * scaled + 1.0 / order
    q_zero = Q_CUT * (1.0 - jnp.exp(-(series * scaled)))
    q_buf[...] = q_zero
    top = jnp.max(q_zero, axis=0, keepdims=True)
    top = jnp.broadcast_to(jnp.max(top, axis=1, keepdims=True), (1, 128))
    top_src[...] = top
    tops[me] = top

    def spread(d, carry):
        p = (me + d * 37) % devices
        send(top_src, tops.at[me], 1, p)
        return carry

    lax.fori_loop(1, devices, spread, 0)
    others = tops.at[pl.ds(0, devices - 1)]
    received(others, 1)
    q_top = jnp.max(tops[...])

    inv_top = 1.0 / jnp.broadcast_to(q_top, (8, 128))
    weight = math.sqrt(3.0) / 6.0

    def theta_rows(r, carry):
        rows = pl.ds(pl.multiple_of(r * 8, 8), 8)
        for lane in range(NZ // 128):
            lanes = pl.ds(lane * 128, 128)
            value = planes[2, rows, lanes] * weight
            position = jnp.maximum(
                (NQ - 1.0) + jnp.log(q_buf[rows, lanes] * inv_top) / STEP, 0.0
            )
            splines = []
            for j in range(-1, NQ + 1):
                offset = jnp.abs(position - float(j))
                wide = jnp.maximum(2.0 - offset, 0.0)
                narrow = jnp.maximum(1.0 - offset, 0.0)
                splines.append(wide * wide * wide - 4.0 * (narrow * narrow * narrow))
            up = [splines[0]]
            for j in range(1, KNOTS - 1):
                up.append(splines[j] + LAM * up[-1])
            down = splines[KNOTS - 1]
            for a in range(NQ - 1, -1, -1):
                below = LAM * down
                thetas[a, rows, lanes] = (up[a + 1] + below) * value
                down = splines[a + 1] + below
        return carry

    lax.fori_loop(0, NY // 8, theta_rows, 0)

    table_yf = ty_f[...]
    my_row, my_cols = me // per_row, pl.ds(pl.multiple_of((me % per_row) * COLS, 128), COLS)
    for c in range(CHUNKS):
        part = pl.ds(c * QC, QC)

        def y_forward(a, carry, c=c):
            mid[a] = left_multiply(table_yf, thetas[c * QC + a])
            return carry

        lax.fori_loop(0, QC, y_forward, 0)
        rows = right_multiply(mid[...].reshape(QC * NY, NZ), tz, False)
        send1[part] = rows.reshape(QC, NY, NZ)

        def lines_out(d, carry, c=c, part=part):
            p = (me + d * 37) % devices
            cols = pl.ds(pl.multiple_of((p % per_row) * COLS, 128), COLS)
            send(send1.at[part, p // per_row, cols], recv1.at[part, me], 2 + c, p)
            return carry

        lax.fori_loop(1, devices, lines_out, 0)
        keep(send1.at[part, my_row, my_cols], recv1.at[part, me], 2 + c)

    wave_y = jnp.where(my_row <= NY // 2, my_row, my_row - NY // 2).astype(F32) * (2.0 * math.pi / NY)
    yz2 = fz2[:, my_cols] + wave_y * wave_y
    top_sq = jnp.broadcast_to(q_top * q_top, (8, COLS))

    def gain_rows(r, carry):
        rows = pl.ds(pl.multiple_of(r * 8, 8), 8)
        line = fx2[rows, :]
        k_sq = jnp.concatenate([line] * (COLS // 128), axis=1) + yz2
        for s in range(SUMS):
            mass = top_sq * math.exp(-STEP * (2 * NQ - 2 - s))
            gain[s, rows, :] = LOCAL + mass / (k_sq + mass)
        return carry

    lax.fori_loop(0, NX // 8, gain_rows, 0)

    table_xf, table_xi = tx_f[...], tx_i[...]
    for c in range(CHUNKS):
        received(recv1.at[pl.ds(c * QC, QC)], 2 + c)

        def x_forward(a, carry, c=c):
            spec[c * QC + a] = left_multiply(table_xf, recv1[c * QC + a])
            return carry

        lax.fori_loop(0, QC, x_forward, 0)

    for c in range(CHUNKS):
        part = pl.ds(c * QC, QC)

        def couple(r, carry, c=c):
            rows = pl.ds(pl.multiple_of(r * 8, 8), 8)
            for lane in range(COLS // 128):
                lanes = pl.ds(lane * 128, 128)
                source = [spec[b, rows, lanes] for b in range(NQ)]
                factor = {}
                for s in range(c * QC, c * QC + QC + NQ - 1):
                    factor[s] = gain[s, rows, lanes]
                for a in range(QC):
                    total = None
                    for b in range(NQ):
                        term = (coup[c * QC + a, b] * factor[c * QC + a + b]) * source[b]
                        total = term if total is None else total + term
                    prod[a, rows, lanes] = total
            return carry

        lax.fori_loop(0, NX // 8, couple, 0)

        def x_inverse(a, carry, c=c):
            send2[c * QC + a] = left_multiply(table_xi, prod[a])
            return carry

        lax.fori_loop(0, QC, x_inverse, 0)

        def lines_back(d, carry, c=c, part=part):
            p = (me + d * 37) % devices
            send(send2.at[part, p], recv2.at[part, my_row, my_cols], 4 + c, p)
            return carry

        lax.fori_loop(1, devices, lines_back, 0)
        keep(send2.at[part, me], recv2.at[part, my_row, my_cols], 4 + c)

    table_yi = ty_i[...]
    here = me % group
    row_x = me % block_x
    for c in range(CHUNKS):
        part = pl.ds(c * QC, QC)
        received(recv2.at[part], 4 + c)
        rows = right_multiply(recv2[part].reshape(QC * NY, NZ), tz, True)
        mid[...] = rows.reshape(QC, NY, NZ)

        def y_inverse(a, carry, c=c):
            send3[c * QC + a] = left_multiply(table_yi, mid[a])
            return carry

        lax.fori_loop(0, QC, y_inverse, 0)

        def block(w):
            ys = pl.ds(pl.multiple_of((w // nz) * block_y, 8), block_y)
            zs = pl.ds(pl.multiple_of((w % nz) * block_z, 128), block_z)
            return send3.at[part, ys, zs]

        def blocks_out(d, carry, c=c, part=part, block=block):
            w = (here + d * 11) % group
            send(block(w), out.at[part, row_x], 6 + c, ix * group + w)
            return carry

        lax.fori_loop(1, group, blocks_out, 0)
        keep(block(here), out.at[part, row_x], 6 + c)

    for c in range(CHUNKS):
        received(out.at[pl.ds(c * QC, QC)], 6 + c)

    sent((5 * block_x - 5) * block_y * block_z // COLS, 0)

    def sent_block(i, carry):
        part = dens.at[0]
        pltpu.make_async_copy(part, part, ssem.at[0]).wait()
        return carry

    edge = jnp.maximum(2 - row_x, 0) + jnp.maximum(row_x - (block_x - 3), 0)
    lax.fori_loop(0, edge, sent_block, 0)
    pltpu.make_async_copy(others, others, ssem.at[1]).wait()
    for c in range(CHUNKS):
        sent((devices - 1) * QC, 2 + c)
        sent((devices - 1) * QC, 4 + c)
        sent((group - 1) * QC * block_y * block_z // COLS, 6 + c)


def solution(mesh):
    sizes = tuple(mesh.shape[axis] for axis in ("gx", "gy", "gz"))
    bz = basis(NZ)
    tz = np.stack(halves(bz))
    by, bx = basis(NY), basis(NX)
    fx2 = np.broadcast_to(wave_squared(NX)[:, None], (NX, 128)).astype(np.float32)
    fz2 = np.broadcast_to(wave_squared(NZ)[None, :], (8, NZ)).astype(np.float32)
    tables = (tz, left_table(by.T), left_table(by), left_table(bx.T), left_table(bx), fx2, fz2)

    def body(density, coupling):
        vmem = pl.BlockSpec(memory_space=pltpu.VMEM)
        block = density.shape
        return pl.pallas_call(
            functools.partial(kernel, sizes),
            out_shape=jax.ShapeDtypeStruct((NQ,) + block, F32),
            in_specs=[vmem, pl.BlockSpec(memory_space=pltpu.SMEM)] + [vmem] * len(tables),
            out_specs=vmem,
            scratch_shapes=[
                pltpu.VMEM((5, NY, NZ), F32),
                pltpu.VMEM((NY, NZ), F32),
                pltpu.VMEM((1, 128), F32),
                pltpu.VMEM((NX, 1, 128), F32),
                pltpu.VMEM((NQ, NY, NZ), F32),
                pltpu.VMEM((QC, NY, NZ), F32),
                pltpu.VMEM((NQ, NY, NZ), F32),
                pltpu.VMEM((NQ, NX, COLS), F32),
                pltpu.VMEM((NQ, NX, COLS), F32),
                pltpu.VMEM((SUMS, NX, COLS), F32),
                pltpu.VMEM((QC, NX, COLS), F32),
                pltpu.VMEM((NQ, NX, COLS), F32),
                pltpu.VMEM((NQ, NY, NZ), F32),
                pltpu.VMEM((NQ, NY, NZ), F32),
                pltpu.SemaphoreType.DMA((8,)),
                pltpu.SemaphoreType.DMA((8,)),
            ],
            compiler_params=pltpu.CompilerParams(
                collective_id=0, has_side_effects=True, vmem_limit_bytes=56 * 1024 * 1024
            ),
            name="convolve",
        )(density, coupling, *[jnp.asarray(t) for t in tables])

    placed = (P("gx", "gy", "gz"), P())
    return jax.shard_map(
        body, mesh=mesh, in_specs=placed, out_specs=P(None, "gx", "gy", "gz"), check_vma=False
    )
```

profile of v0, /device:TPU:1, one launch (start us, length us, event | category | flops | bytes accessed | tf_op | source)
XLA Modules:
  0.0 111.5 jit_solution(10819245996360312501)
XLA Ops:
  0.0 108.6 %convolve.1 = f32[14,16,16,128]{3,2,1,0:T(8,128)} custom-call(f32[16,16,128]{2,1,0:T(8,128)} %dens.1, f32[14,14]{1,0:T(8,128)} %coup.1, bf16[2,512,512]{2,1,0:T(8,128)(2,1)} %constant.14.clone.tz, bf16[64,192]{1,0:T(8,128)(2,1)} %constant.15.clone.ty_f, bf16[64,192]{1,0:T(8,128)(2,1)} %constant.16.clone.ty_i, bf16[128,384]{1,0:T(8,128)(2,1)} %constant.17.clone.tx_f, ...), custom_call_target="tpu_custom_call" | custom-call | tf_op jit(solution)/shard_map/convolve/pallas_call | solution.py:354
  108.6 2.9 %copy.11 = f32[14,16,16,128]{3,2,1,0:T(8,128)} copy(f32[14,16,16,128]{3,2,1,0:T(8,128)} %convolve.1) | data formatting | bytes 3670016
where the time goes:
time: 112 us
  Pallas kernels  109 us (97%)
  local copies, waits for them, and re-layouts  2.88 us (3%)
    pallas_call x1, Pallas kernels, body(): pl.pallas_call(functools.partial(kernel, sizes), out_shape=jax.ShapeDtype...  109 us
    unnamed x1, local copies, waits for them, and re-layouts  2.88 us

commit v1 on v0

--- a/solution.py
+++ b/solution.py
@@ -91,7 +91,8 @@
     per_row = NZ // COLS
 
     def ids(p):
-        return {"gx": p // group, "gy": (p // nz) % ny, "gz": p % nz}
+        rest = lax.rem(p, group)
+        return {"gx": lax.div(p, group), "gy": lax.div(rest, nz), "gz": lax.rem(rest, nz)}
 
     def send(src, dst, slot, p):
         pltpu.make_async_remote_copy(
@@ -119,7 +120,7 @@
     barrier = pltpu.get_barrier_semaphore()
 
     def greet(d, carry):
-        p = (me + d) % devices
+        p = lax.rem(me + d, devices)
         pl.semaphore_signal(barrier, inc=1, device_id=ids(p), device_id_type=MESH)
         return carry
 
@@ -131,8 +132,8 @@
     for shift in range(5):
 
         def give(r, carry, shift=shift):
-            row = (me + r * 5 + shift) % block_x
-            p = (ix * block_x + row - (shift - 2) + devices) % devices
+            row = lax.rem(me + r * 5 + shift, block_x)
+            p = lax.rem(ix * block_x + row - (shift - 2) + devices, devices)
             src, dst = dens.at[row], planes.at[shift, here_y, here_z]
 
             @pl.when(p != me)
@@ -172,7 +173,7 @@
     tops[me] = top
 
     def spread(d, carry):
-        p = (me + d * 37) % devices
+        p = lax.rem(me + d * 37, devices)
         send(top_src, tops.at[me], 1, p)
         return carry
 
@@ -211,7 +212,7 @@
     lax.fori_loop(0, NY // 8, theta_rows, 0)
 
     table_yf = ty_f[...]
-    my_row, my_cols = me // per_row, pl.ds(pl.multiple_of((me % per_row) * COLS, 128), COLS)
+    my_row, my_cols = lax.div(me, per_row), pl.ds(pl.multiple_of(lax.rem(me, per_row) * COLS, 128), COLS)
     for c in range(CHUNKS):
         part = pl.ds(c * QC, QC)
 
@@ -224,9 +225,9 @@
         send1[part] = rows.reshape(QC, NY, NZ)
 
         def lines_out(d, carry, c=c, part=part):
-            p = (me + d * 37) % devices
-            cols = pl.ds(pl.multiple_of((p % per_row) * COLS, 128), COLS)
-            send(send1.at[part, p // per_row, cols], recv1.at[part, me], 2 + c, p)
+            p = lax.rem(me + d * 37, devices)
+            cols = pl.ds(pl.multiple_of(lax.rem(p, per_row) * COLS, 128), COLS)
+            send(send1.at[part, lax.div(p, per_row), cols], recv1.at[part, me], 2 + c, p)
             return carry
 
         lax.fori_loop(1, devices, lines_out, 0)
@@ -285,7 +286,7 @@
         lax.fori_loop(0, QC, x_inverse, 0)
 
         def lines_back(d, carry, c=c, part=part):
-            p = (me + d * 37) % devices
+            p = lax.rem(me + d * 37, devices)
             send(send2.at[part, p], recv2.at[part, my_row, my_cols], 4 + c, p)
             return carry
 
@@ -293,8 +294,8 @@
         keep(send2.at[part, me], recv2.at[part, my_row, my_cols], 4 + c)
 
     table_yi = ty_i[...]
-    here = me % group
-    row_x = me % block_x
+    here = lax.rem(me, group)
+    row_x = lax.rem(me, block_x)
     for c in range(CHUNKS):
         part = pl.ds(c * QC, QC)
         received(recv2.at[part], 4 + c)
@@ -308,12 +309,12 @@
         lax.fori_loop(0, QC, y_inverse, 0)
 
         def block(w):
-            ys = pl.ds(pl.multiple_of((w // nz) * block_y, 8), block_y)
-            zs = pl.ds(pl.multiple_of((w % nz) * block_z, 128), block_z)
+            ys = pl.ds(pl.multiple_of(lax.div(w, nz) * block_y, 8), block_y)
+            zs = pl.ds(pl.multiple_of(lax.rem(w, nz) * block_z, 128), block_z)
             return send3.at[part, ys, zs]
 
         def blocks_out(d, carry, c=c, part=part, block=block):
-            w = (here + d * 11) % group
+            w = lax.rem(here + d * 11, group)
             send(block(w), out.at[part, row_x], 6 + c, ix * group + w)
             return carry
 

time: 112 us -> 110 us (0.982)
  Pallas kernels: 109 us -> 107 us
    pallas_call x1, Pallas kernels: 109 us -> 107 us  [body(): pl.pallas_call(functools.partial(kernel, sizes), out_shape=jax.ShapeDtype...]
where the time goes in v1:
time: 110 us
  Pallas kernels  107 us (97%)
  local copies, waits for them, and re-layouts  2.88 us (3%)
    pallas_call x1, Pallas kernels, body(): pl.pallas_call(functools.partial(kernel, sizes), out_shape=jax.ShapeDtype...  107 us
    unnamed x1, local copies, waits for them, and re-layouts  2.88 us

profile of v1, /device:TPU:1, one launch (start us, length us, event | category | flops | bytes accessed | tf_op | source)
XLA Modules:
  0.0 109.9 jit_solution(2114319180352064338)
XLA Ops:
  0.0 107.1 %convolve.1 = f32[14,16,16,128]{3,2,1,0:T(8,128)} custom-call(f32[16,16,128]{2,1,0:T(8,128)} %dens.1, f32[14,14]{1,0:T(8,128)} %coup.1, bf16[2,512,512]{2,1,0:T(8,128)(2,1)} %constant.14.clone.tz, bf16[64,192]{1,0:T(8,128)(2,1)} %constant.15.clone.ty_f, bf16[64,192]{1,0:T(8,128)(2,1)} %constant.16.clone.ty_i, bf16[128,384]{1,0:T(8,128)(2,1)} %constant.17.clone.tx_f, ...), custom_call_target="tpu_custom_call" | custom-call | tf_op jit(solution)/shard_map/convolve/pallas_call | solution.py:355
  107.1 2.9 %copy.11 = f32[14,16,16,128]{3,2,1,0:T(8,128)} copy(f32[14,16,16,128]{3,2,1,0:T(8,128)} %convolve.1) | data formatting | bytes 3670016

commit v2 on v1

--- a/solution.py
+++ b/solution.py
@@ -79,8 +79,8 @@
 
 def kernel(
     sizes, dens, coup, tz, ty_f, ty_i, tx_f, tx_i, fx2, fz2, out,
-    planes, q_buf, top_src, tops, thetas, mid, send1, recv1, spec, gain, prod, send2, recv2, send3,
-    ssem, rsem,
+    ext, zext, zsend, zhalo, planes, q_buf, top_src, near_tops, far_tops, thetas, mid, send1, recv1, spec, gain, prod, send2, recv2, send3,
+    ssem, rsem, hsend, hrecv,
 ):
     devices = NX
     nx, ny, nz = sizes
@@ -90,13 +90,9 @@
     block_x, block_y, block_z = NX // nx, NY // ny, NZ // nz
     per_row = NZ // COLS
 
-    def ids(p):
-        rest = lax.rem(p, group)
-        return {"gx": lax.div(p, group), "gy": lax.div(rest, nz), "gz": lax.rem(rest, nz)}
-
-    def send(src, dst, slot, p):
+    def send(src, dst, slot, to):
         pltpu.make_async_remote_copy(
-            src, dst, ssem.at[slot], rsem.at[slot], device_id=ids(p), device_id_type=MESH
+            src, dst, ssem.at[slot], rsem.at[slot], device_id=to, device_id_type=MESH
         ).start()
 
     def keep(src, dst, slot):
@@ -117,70 +113,106 @@
             part = recv1.at[0, 0]
             pltpu.make_async_copy(part, part, ssem.at[slot]).wait()
 
+    block = dens[...]
+    ext[pl.ds(2, block_x), pl.ds(8, block_y), :] = block
+    turned = block.reshape(block_x * block_y, block_z).T
+    zext[pl.ds(8, block_z), :] = turned
+    zsend[0] = turned[:2]
+    zsend[1] = turned[block_z - 2 :]
+
+    gys = [lax.rem(iy + j, ny) for j in range(ny)]
+    gzs = [lax.rem(iz + j, nz) for j in range(nz)]
+    near = [(dy, dz) for dz in range(nz) for dy in range(ny)]
     barrier = pltpu.get_barrier_semaphore()
-
-    def greet(d, carry):
-        p = lax.rem(me + d, devices)
-        pl.semaphore_signal(barrier, inc=1, device_id=ids(p), device_id_type=MESH)
-        return carry
-
-    lax.fori_loop(1, devices, greet, 0)
-    pl.semaphore_wait(barrier, devices - 1)
-
+    for dy, dz in near[1:]:
+        pl.semaphore_signal(
+            barrier, inc=1, device_id={"gy": gys[dy], "gz": gzs[dz]}, device_id_type=MESH
+        )
+    for dx in range(1, nx):
+        pl.semaphore_signal(
+            barrier, inc=1, device_id={"gx": lax.rem(ix + dx, nx)}, device_id_type=MESH
+        )
+    pl.semaphore_wait(barrier, group - 1 + nx - 1)
+
+    halos = []
+
+    def halo(src, dst, to):
+        slot = len(halos)
+        copy = pltpu.make_async_remote_copy(
+            src, dst, hsend.at[slot], hrecv.at[slot], device_id=to, device_id_type=MESH
+        )
+        copy.start()
+        halos.append(copy)
+
+    low_x, high_x = {"gx": lax.rem(ix + nx - 1, nx)}, {"gx": lax.rem(ix + 1, nx)}
+    low_y, high_y = {"gy": gys[ny - 1]}, {"gy": gys[1]}
+    low_z, high_z = {"gz": gzs[nz - 1]}, {"gz": gzs[1]}
+    inner_x, inner_y = pl.ds(2, block_x), pl.ds(8, block_y)
+    halo(dens.at[pl.ds(0, 2)], ext.at[pl.ds(block_x + 2, 2), inner_y], low_x)
+    halo(dens.at[pl.ds(block_x - 2, 2)], ext.at[pl.ds(0, 2), inner_y], high_x)
+    for k in range(2):
+        halo(dens.at[:, k, :], ext.at[inner_x, block_y + 8 + k, :], low_y)
+        halo(dens.at[:, block_y - 2 + k, :], ext.at[inner_x, 6 + k, :], high_y)
+    halo(zsend.at[0], zhalo.at[1], low_z)
+    halo(zsend.at[1], zhalo.at[0], high_z)
+
+    here, row_x = iy * nz + iz, iy * nz + iz
     here_y = pl.ds(pl.multiple_of(iy * block_y, 8), block_y)
     here_z = pl.ds(pl.multiple_of(iz * block_z, 128), block_z)
-    for shift in range(5):
-
-        def give(r, carry, shift=shift):
-            row = lax.rem(me + r * 5 + shift, block_x)
-            p = lax.rem(ix * block_x + row - (shift - 2) + devices, devices)
-            src, dst = dens.at[row], planes.at[shift, here_y, here_z]
-
-            @pl.when(p != me)
-            def _():
-                send(src, dst, 0, p)
-
-            @pl.when(p == me)
-            def _():
-                keep(src, dst, 0)
-
-            return carry
-
-        lax.fori_loop(0, block_x, give, 0)
-    received(planes, 0)
-
-    own = planes[2]
-    slope_x = (8.0 * (planes[3] - planes[1]) - (planes[4] - planes[0])) / 12.0
-    grad_sq = slope_x * slope_x
-    for axis, length in ((0, NY), (1, NZ)):
-        nearer = pltpu.roll(own, length - 1, axis) - pltpu.roll(own, 1, axis)
-        farther = pltpu.roll(own, length - 2, axis) - pltpu.roll(own, 2, axis)
-        slope = (8.0 * nearer - farther) / 12.0
-        grad_sq = grad_sq + slope * slope
-    cube = (3.0 * math.pi * math.pi) * own
+
+    def rows_out(src, which):
+        for dy, dz in near:
+            row = gys[dy] * nz + gzs[dz]
+            dst = planes.at[which, here_y, here_z]
+            if dy or dz:
+                send(src.at[row], dst, 0, {"gy": gys[dy], "gz": gzs[dz]})
+            else:
+                keep(src.at[row], dst, 0)
+
+    rows_out(dens, 0)
+    for copy in halos:
+        copy.wait()
+
+    zext[6:8, :] = zhalo[0]
+    zext[pl.ds(block_z + 8, 2), :] = zhalo[1]
+
+    def squared_slope(at):
+        slope = (8.0 * (at(1) - at(-1)) - (at(2) - at(-2))) / 12.0
+        return slope * slope
+
+    grad_sq = squared_slope(lambda o: ext[pl.ds(2 + o, block_x), inner_y, :])
+    grad_sq = grad_sq + squared_slope(lambda o: ext[inner_x, pl.ds(8 + o, block_y), :])
+    along_z = squared_slope(lambda o: zext[pl.ds(8 + o, block_z), :])
+    grad_sq = grad_sq + along_z.T.reshape(block_x, block_y, block_z)
+    cube = (3.0 * math.pi * math.pi) * block
     fermi_k = jnp.exp(jnp.log(cube) / 3.0)
     fermi_k = fermi_k - (fermi_k - cube / (fermi_k * fermi_k)) * (1.0 / 3.0)
-    reduced = grad_sq / (4.0 * fermi_k * fermi_k * own * own)
+    reduced = grad_sq / (4.0 * fermi_k * fermi_k * block * block)
     scaled = fermi_k * (1.0 + ZAB * reduced) / Q_CUT
     series = jnp.full_like(scaled, 1.0 / 12.0)
     for order in range(11, 0, -1):
         series = series * scaled + 1.0 / order
     q_zero = Q_CUT * (1.0 - jnp.exp(-(series * scaled)))
     q_buf[...] = q_zero
-    top = jnp.max(q_zero, axis=0, keepdims=True)
+    top = jnp.max(jnp.max(q_zero, axis=0), axis=0, keepdims=True)
     top = jnp.broadcast_to(jnp.max(top, axis=1, keepdims=True), (1, 128))
-    top_src[...] = top
-    tops[me] = top
-
-    def spread(d, carry):
-        p = lax.rem(me + d * 37, devices)
-        send(top_src, tops.at[me], 1, p)
-        return carry
-
-    lax.fori_loop(1, devices, spread, 0)
-    others = tops.at[pl.ds(0, devices - 1)]
+    top_src[0] = top
+    near_tops[here] = top
+
+    for dy, dz in near[1:]:
+        send(top_src.at[0], near_tops.at[here], 1, {"gy": gys[dy], "gz": gzs[dz]})
+    rows_out(q_buf, 1)
+    others = near_tops.at[pl.ds(0, group - 1)]
     received(others, 1)
-    q_top = jnp.max(tops[...])
+    top = jnp.max(near_tops[...], axis=0)
+    top_src[1] = top
+    far_tops[ix] = top
+    for dx in range(1, nx):
+        send(top_src.at[1], far_tops.at[ix], 8, {"gx": lax.rem(ix + dx, nx)})
+    far_others = far_tops.at[pl.ds(0, nx - 1)]
+    received(far_others, 8)
+    q_top = jnp.max(far_tops[...])
+    received(planes, 0)
 
     inv_top = 1.0 / jnp.broadcast_to(q_top, (8, 128))
     weight = math.sqrt(3.0) / 6.0
@@ -189,9 +221,9 @@
         rows = pl.ds(pl.multiple_of(r * 8, 8), 8)
         for lane in range(NZ // 128):
             lanes = pl.ds(lane * 128, 128)
-            value = planes[2, rows, lanes] * weight
+            value = planes[0, rows, lanes] * weight
             position = jnp.maximum(
-                (NQ - 1.0) + jnp.log(q_buf[rows, lanes] * inv_top) / STEP, 0.0
+                (NQ - 1.0) + jnp.log(planes[1, rows, lanes] * inv_top) / STEP, 0.0
             )
             splines = []
             for j in range(-1, NQ + 1):
@@ -212,6 +244,26 @@
     lax.fori_loop(0, NY // 8, theta_rows, 0)
 
     table_yf = ty_f[...]
+    rows_of = [lax.div(g, per_row) for g in gzs]
+    cols_of = [pl.ds(pl.multiple_of(lax.rem(g, per_row) * COLS, 128), COLS) for g in gzs]
+    spread = [near[(m * 7) % group] for m in range(group)]
+
+    def to_all(issue):
+        def step(t, carry):
+            for m, (dy, dz) in enumerate(spread):
+                gx = lax.rem(ix + t + 3 * m, nx)
+                p = (gx * ny + gys[dy]) * nz + gzs[dz]
+                row = (gx * ny + gys[dy]) * (nz // per_row) + rows_of[dz]
+                to = {"gx": gx, "gy": gys[dy], "gz": gzs[dz]}
+                run = functools.partial(issue, p, row, cols_of[dz], to)
+                if dy or dz:
+                    run()
+                else:
+                    pl.when(t != (nx - 3 * m) % nx)(run)
+            return carry
+
+        lax.fori_loop(0, nx, step, 0)
+
     my_row, my_cols = lax.div(me, per_row), pl.ds(pl.multiple_of(lax.rem(me, per_row) * COLS, 128), COLS)
     for c in range(CHUNKS):
         part = pl.ds(c * QC, QC)
@@ -224,13 +276,7 @@
         rows = right_multiply(mid[...].reshape(QC * NY, NZ), tz, False)
         send1[part] = rows.reshape(QC, NY, NZ)
 
-        def lines_out(d, carry, c=c, part=part):
-            p = lax.rem(me + d * 37, devices)
-            cols = pl.ds(pl.multiple_of(lax.rem(p, per_row) * COLS, 128), COLS)
-            send(send1.at[part, lax.div(p, per_row), cols], recv1.at[part, me], 2 + c, p)
-            return carry
-
-        lax.fori_loop(1, devices, lines_out, 0)
+        to_all(lambda p, row, cols, to: send(send1.at[part, row, cols], recv1.at[part, me], 2 + c, to))
         keep(send1.at[part, my_row, my_cols], recv1.at[part, me], 2 + c)
 
     wave_y = jnp.where(my_row <= NY // 2, my_row, my_row - NY // 2).astype(F32) * (2.0 * math.pi / NY)
@@ -285,17 +331,10 @@
 
         lax.fori_loop(0, QC, x_inverse, 0)
 
-        def lines_back(d, carry, c=c, part=part):
-            p = lax.rem(me + d * 37, devices)
-            send(send2.at[part, p], recv2.at[part, my_row, my_cols], 4 + c, p)
-            return carry
-
-        lax.fori_loop(1, devices, lines_back, 0)
+        to_all(lambda p, row, cols, to: send(send2.at[part, p], recv2.at[part, my_row, my_cols], 4 + c, to))
         keep(send2.at[part, me], recv2.at[part, my_row, my_cols], 4 + c)
 
     table_yi = ty_i[...]
-    here = lax.rem(me, group)
-    row_x = lax.rem(me, block_x)
     for c in range(CHUNKS):
         part = pl.ds(c * QC, QC)
         received(recv2.at[part], 4 + c)
@@ -308,32 +347,21 @@
 
         lax.fori_loop(0, QC, y_inverse, 0)
 
-        def block(w):
-            ys = pl.ds(pl.multiple_of(lax.div(w, nz) * block_y, 8), block_y)
-            zs = pl.ds(pl.multiple_of(lax.rem(w, nz) * block_z, 128), block_z)
-            return send3.at[part, ys, zs]
-
-        def blocks_out(d, carry, c=c, part=part, block=block):
-            w = lax.rem(here + d * 11, group)
-            send(block(w), out.at[part, row_x], 6 + c, ix * group + w)
-            return carry
-
-        lax.fori_loop(1, group, blocks_out, 0)
-        keep(block(here), out.at[part, row_x], 6 + c)
+        for dy, dz in near:
+            ys = pl.ds(pl.multiple_of(gys[dy] * block_y, 8), block_y)
+            zs = pl.ds(pl.multiple_of(gzs[dz] * block_z, 128), block_z)
+            src, dst = send3.at[part, ys, zs], out.at[part, row_x]
+            if dy or dz:
+                send(src, dst, 6 + c, {"gy": gys[dy], "gz": gzs[dz]})
+            else:
+                keep(src, dst, 6 + c)
 
     for c in range(CHUNKS):
         received(out.at[pl.ds(c * QC, QC)], 6 + c)
 
-    sent((5 * block_x - 5) * block_y * block_z // COLS, 0)
-
-    def sent_block(i, carry):
-        part = dens.at[0]
-        pltpu.make_async_copy(part, part, ssem.at[0]).wait()
-        return carry
-
-    edge = jnp.maximum(2 - row_x, 0) + jnp.maximum(row_x - (block_x - 3), 0)
-    lax.fori_loop(0, edge, sent_block, 0)
+    sent(2 * (group - 1) * block_y * block_z // COLS, 0)
     pltpu.make_async_copy(others, others, ssem.at[1]).wait()
+    pltpu.make_async_copy(far_others, far_others, ssem.at[8]).wait()
     for c in range(CHUNKS):
         sent((devices - 1) * QC, 2 + c)
         sent((devices - 1) * QC, 4 + c)
@@ -358,10 +386,15 @@
             in_specs=[vmem, pl.BlockSpec(memory_space=pltpu.SMEM)] + [vmem] * len(tables),
             out_specs=vmem,
             scratch_shapes=[
-                pltpu.VMEM((5, NY, NZ), F32),
-                pltpu.VMEM((NY, NZ), F32),
-                pltpu.VMEM((1, 128), F32),
-                pltpu.VMEM((NX, 1, 128), F32),
+                pltpu.VMEM((block[0] + 4, block[1] + 16, block[2]), F32),
+                pltpu.VMEM((block[2] + 16, block[0] * block[1]), F32),
+                pltpu.VMEM((2, 2, block[0] * block[1]), F32),
+                pltpu.VMEM((2, 2, block[0] * block[1]), F32),
+                pltpu.VMEM((2, NY, NZ), F32),
+                pltpu.VMEM(block, F32),
+                pltpu.VMEM((2, 1, 128), F32),
+                pltpu.VMEM((sizes[1] * sizes[2], 1, 128), F32),
+                pltpu.VMEM((sizes[0], 1, 128), F32),
                 pltpu.VMEM((NQ, NY, NZ), F32),
                 pltpu.VMEM((QC, NY, NZ), F32),
                 pltpu.VMEM((NQ, NY, NZ), F32),
@@ -372,6 +405,8 @@
                 pltpu.VMEM((NQ, NX, COLS), F32),
                 pltpu.VMEM((NQ, NY, NZ), F32),
                 pltpu.VMEM((NQ, NY, NZ), F32),
+                pltpu.SemaphoreType.DMA((9,)),
+                pltpu.SemaphoreType.DMA((9,)),
                 pltpu.SemaphoreType.DMA((8,)),
                 pltpu.SemaphoreType.DMA((8,)),
             ],

time: 110 us -> 101 us (0.918)
  Pallas kernels: 107 us -> 98.1 us
    pallas_call x1, Pallas kernels: 107 us -> 98.1 us  [body(): pl.pallas_call(functools.partial(kernel, sizes), out_shape=jax.ShapeDtype...]
where the time goes in v2:
time: 101 us
  Pallas kernels  98.1 us (97%)
  local copies, waits for them, and re-layouts  2.88 us (3%)
    pallas_call x1, Pallas kernels, body(): pl.pallas_call(functools.partial(kernel, sizes), out_shape=jax.ShapeDtype...  98.1 us
    unnamed x1, local copies, waits for them, and re-layouts  2.88 us

profile of v2, /device:TPU:1, one launch (start us, length us, event | category | flops | bytes accessed | tf_op | source)
XLA Modules:
  0.0 101.0 jit_solution(10464422522837539273)
XLA Ops:
  0.0 98.1 %convolve.1 = f32[14,16,16,128]{3,2,1,0:T(8,128)} custom-call(f32[16,16,128]{2,1,0:T(8,128)} %dens.1, f32[14,14]{1,0:T(8,128)} %coup.1, bf16[2,512,512]{2,1,0:T(8,128)(2,1)} %constant.14.clone.tz, bf16[64,192]{1,0:T(8,128)(2,1)} %constant.15.clone.ty_f, bf16[64,192]{1,0:T(8,128)(2,1)} %constant.16.clone.ty_i, bf16[128,384]{1,0:T(8,128)(2,1)} %constant.17.clone.tx_f, ...), custom_call_target="tpu_custom_call" | custom-call | tf_op jit(solution)/shard_map/convolve/pallas_call | solution.py:383
  98.1 2.9 %copy.11 = f32[14,16,16,128]{3,2,1,0:T(8,128)} copy(f32[14,16,16,128]{3,2,1,0:T(8,128)} %convolve.1) | data formatting | bytes 3670016

commit v3 on v2

--- a/solution.py
+++ b/solution.py
@@ -15,8 +15,8 @@
 
 NQ = 14
 NX, NY, NZ = 128, 64, 512
-CHUNKS = 2
-QC = NQ // CHUNKS
+FORWARD = (5, 9)
+BACKWARD = (4, 5, 5)
 KNOTS = NQ + 2
 COLS = NY * NZ // NX
 SUMS = 2 * NQ - 1
@@ -26,6 +26,10 @@
 STEP = 0.07
 LOCAL = 0.25
 LAM = math.sqrt(3.0) - 2.0
+FIRST_LINES, FIRST_BACK = 3, 3 + len(FORWARD)
+FIRST_OUT = FIRST_BACK + len(BACKWARD)
+SLOTS = FIRST_OUT + len(BACKWARD)
+Y_SCALE = math.sqrt(2.0 / NY)
 
 
 def frequencies(length):
@@ -44,6 +48,26 @@
     return table * scale
 
 
+def spans(counts):
+    starts = [sum(counts[:k]) for k in range(len(counts))]
+    return list(enumerate(zip(starts, counts)))
+
+
+def hops(offset):
+    dx, dy, dz = offset
+    along_y = (0, 1, 2, 1)[dx // 4 * 2 + dz // 2]
+    return min(dy, 4 - dy) + min(dx % 4, 4 - dx % 4) + along_y
+
+
+def far_first():
+    offsets = [(dx, dy, dz) for dx in range(8) for dy in range(4) for dz in range(4)][1:]
+    shuffled = [offsets[k] for k in np.random.RandomState(3).permutation(len(offsets))]
+    return sorted(shuffled, key=lambda offset: -hops(offset))
+
+
+ORDER = far_first()
+
+
 def halves(table):
     high = table.astype(BF16)
     low = (table - high.astype(np.float64)).astype(BF16)
@@ -55,8 +79,10 @@
     return np.concatenate([high, high, low], axis=1)
 
 
-def wave_squared(length):
-    return (2.0 * np.pi / length * frequencies(length)) ** 2
+def wave_squared(index, length):
+    wave = jnp.where(index <= length // 2, index, index - length // 2).astype(F32)
+    wave = wave * (2.0 * math.pi / length)
+    return wave * wave
 
 
 def split(value):
@@ -78,9 +104,9 @@
 
 
 def kernel(
-    sizes, dens, coup, tz, ty_f, ty_i, tx_f, tx_i, fx2, fz2, out,
+    sizes, dens, coup, tz_hbm, ty_f, ty_i, tx_f, tx_i, out,
     ext, zext, zsend, zhalo, planes, q_buf, top_src, near_tops, far_tops, thetas, mid, send1, recv1, spec, gain, prod, send2, recv2, send3,
-    ssem, rsem, hsend, hrecv,
+    tz, table_sem, ssem, rsem, hsend, hrecv,
 ):
     devices = NX
     nx, ny, nz = sizes
@@ -113,15 +139,18 @@
             part = recv1.at[0, 0]
             pltpu.make_async_copy(part, part, ssem.at[slot]).wait()
 
-    block = dens[...]
-    ext[pl.ds(2, block_x), pl.ds(8, block_y), :] = block
-    turned = block.reshape(block_x * block_y, block_z).T
-    zext[pl.ds(8, block_z), :] = turned
-    zsend[0] = turned[:2]
-    zsend[1] = turned[block_z - 2 :]
-
+    load_table = pltpu.make_async_copy(tz_hbm, tz, table_sem)
+    load_table.start()
+    z_len = nx // 2
+    y_hi, z_at, y_lo, core = lax.div(ix, z_len), lax.rem(ix, z_len), lax.div(iz, 2), lax.rem(iz, 2)
     gys = [lax.rem(iy + j, ny) for j in range(ny)]
-    gzs = [lax.rem(iz + j, nz) for j in range(nz)]
+    gzs = [
+        (1 - y_lo if j // 2 else y_lo) * 2 + (1 - core if j % 2 else core) for j in range(nz)
+    ]
+    gxs = [
+        (1 - y_hi if j // z_len else y_hi) * z_len + lax.rem(z_at + j % z_len, z_len)
+        for j in range(nx)
+    ]
     near = [(dy, dz) for dz in range(nz) for dy in range(ny)]
     barrier = pltpu.get_barrier_semaphore()
     for dy, dz in near[1:]:
@@ -130,8 +159,14 @@
         )
     for dx in range(1, nx):
         pl.semaphore_signal(
-            barrier, inc=1, device_id={"gx": lax.rem(ix + dx, nx)}, device_id_type=MESH
+            barrier, inc=1, device_id={"gx": gxs[dx]}, device_id_type=MESH
         )
+    block = dens[...]
+    ext[pl.ds(2, block_x), pl.ds(8, block_y), :] = block
+    turned = block.reshape(block_x * block_y, block_z).T
+    zext[pl.ds(8, block_z), :] = turned
+    zsend[0] = turned[:2]
+    zsend[1] = turned[block_z - 2 :]
     pl.semaphore_wait(barrier, group - 1 + nx - 1)
 
     halos = []
@@ -146,7 +181,7 @@
 
     low_x, high_x = {"gx": lax.rem(ix + nx - 1, nx)}, {"gx": lax.rem(ix + 1, nx)}
     low_y, high_y = {"gy": gys[ny - 1]}, {"gy": gys[1]}
-    low_z, high_z = {"gz": gzs[nz - 1]}, {"gz": gzs[1]}
+    low_z, high_z = {"gz": lax.rem(iz + nz - 1, nz)}, {"gz": lax.rem(iz + 1, nz)}
     inner_x, inner_y = pl.ds(2, block_x), pl.ds(8, block_y)
     halo(dens.at[pl.ds(0, 2)], ext.at[pl.ds(block_x + 2, 2), inner_y], low_x)
     halo(dens.at[pl.ds(block_x - 2, 2)], ext.at[pl.ds(0, 2), inner_y], high_x)
@@ -169,7 +204,6 @@
             else:
                 keep(src.at[row], dst, 0)
 
-    rows_out(dens, 0)
     for copy in halos:
         copy.wait()
 
@@ -202,15 +236,16 @@
     for dy, dz in near[1:]:
         send(top_src.at[0], near_tops.at[here], 1, {"gy": gys[dy], "gz": gzs[dz]})
     rows_out(q_buf, 1)
+    rows_out(dens, 0)
     others = near_tops.at[pl.ds(0, group - 1)]
     received(others, 1)
     top = jnp.max(near_tops[...], axis=0)
     top_src[1] = top
     far_tops[ix] = top
     for dx in range(1, nx):
-        send(top_src.at[1], far_tops.at[ix], 8, {"gx": lax.rem(ix + dx, nx)})
+        send(top_src.at[1], far_tops.at[ix], 2, {"gx": gxs[dx]})
     far_others = far_tops.at[pl.ds(0, nx - 1)]
-    received(far_others, 8)
+    received(far_others, 2)
     q_top = jnp.max(far_tops[...])
     received(planes, 0)
 
@@ -244,49 +279,39 @@
     lax.fori_loop(0, NY // 8, theta_rows, 0)
 
     table_yf = ty_f[...]
+    load_table.wait()
     rows_of = [lax.div(g, per_row) for g in gzs]
     cols_of = [pl.ds(pl.multiple_of(lax.rem(g, per_row) * COLS, 128), COLS) for g in gzs]
-    spread = [near[(m * 7) % group] for m in range(group)]
 
     def to_all(issue):
-        def step(t, carry):
-            for m, (dy, dz) in enumerate(spread):
-                gx = lax.rem(ix + t + 3 * m, nx)
-                p = (gx * ny + gys[dy]) * nz + gzs[dz]
-                row = (gx * ny + gys[dy]) * (nz // per_row) + rows_of[dz]
-                to = {"gx": gx, "gy": gys[dy], "gz": gzs[dz]}
-                run = functools.partial(issue, p, row, cols_of[dz], to)
-                if dy or dz:
-                    run()
-                else:
-                    pl.when(t != (nx - 3 * m) % nx)(run)
+        for dx, dy, dz in ORDER:
+            p = (gxs[dx] * ny + gys[dy]) * nz + gzs[dz]
+            row = (gxs[dx] * ny + gys[dy]) * (nz // per_row) + rows_of[dz]
+            issue(p, row, cols_of[dz], {"gx": gxs[dx], "gy": gys[dy], "gz": gzs[dz]})
+
+    my_row, my_cols = lax.div(me, per_row), pl.ds(pl.multiple_of(lax.rem(me, per_row) * COLS, 128), COLS)
+    for c, (first, count) in spans(FORWARD):
+        part = pl.ds(first, count)
+
+        def y_forward(a, carry, first=first):
+            mid[a] = left_multiply(table_yf, thetas[first + a])
             return carry
 
-        lax.fori_loop(0, nx, step, 0)
-
-    my_row, my_cols = lax.div(me, per_row), pl.ds(pl.multiple_of(lax.rem(me, per_row) * COLS, 128), COLS)
-    for c in range(CHUNKS):
-        part = pl.ds(c * QC, QC)
-
-        def y_forward(a, carry, c=c):
-            mid[a] = left_multiply(table_yf, thetas[c * QC + a])
-            return carry
-
-        lax.fori_loop(0, QC, y_forward, 0)
-        rows = right_multiply(mid[...].reshape(QC * NY, NZ), tz, False)
-        send1[part] = rows.reshape(QC, NY, NZ)
-
-        to_all(lambda p, row, cols, to: send(send1.at[part, row, cols], recv1.at[part, me], 2 + c, to))
-        keep(send1.at[part, my_row, my_cols], recv1.at[part, me], 2 + c)
-
-    wave_y = jnp.where(my_row <= NY // 2, my_row, my_row - NY // 2).astype(F32) * (2.0 * math.pi / NY)
-    yz2 = fz2[:, my_cols] + wave_y * wave_y
+        lax.fori_loop(0, count, y_forward, 0, unroll=True)
+        rows = right_multiply(mid[pl.ds(0, count)].reshape(count * NY, NZ), tz, False)
+        send1[part] = rows.reshape(count, NY, NZ)
+
+        slot = FIRST_LINES + c
+        to_all(lambda p, row, cols, to: send(send1.at[part, row, cols], recv1.at[part, me], slot, to))
+        keep(send1.at[part, my_row, my_cols], recv1.at[part, me], slot)
+
+    col = lax.broadcasted_iota(jnp.int32, (8, COLS), 1) + lax.rem(me, per_row) * COLS
+    yz2 = wave_squared(my_row, NY) + wave_squared(col, NZ)
     top_sq = jnp.broadcast_to(q_top * q_top, (8, COLS))
 
     def gain_rows(r, carry):
         rows = pl.ds(pl.multiple_of(r * 8, 8), 8)
-        line = fx2[rows, :]
-        k_sq = jnp.concatenate([line] * (COLS // 128), axis=1) + yz2
+        k_sq = wave_squared(lax.broadcasted_iota(jnp.int32, (8, COLS), 0) + r * 8, NX) + yz2
         for s in range(SUMS):
             mass = top_sq * math.exp(-STEP * (2 * NQ - 2 - s))
             gain[s, rows, :] = LOCAL + mass / (k_sq + mass)
@@ -295,77 +320,79 @@
     lax.fori_loop(0, NX // 8, gain_rows, 0)
 
     table_xf, table_xi = tx_f[...], tx_i[...]
-    for c in range(CHUNKS):
-        received(recv1.at[pl.ds(c * QC, QC)], 2 + c)
-
-        def x_forward(a, carry, c=c):
-            spec[c * QC + a] = left_multiply(table_xf, recv1[c * QC + a])
+    for c, (first, count) in spans(FORWARD):
+        received(recv1.at[pl.ds(first, count)], FIRST_LINES + c)
+
+        def x_forward(a, carry, first=first):
+            spec[first + a] = left_multiply(table_xf, recv1[first + a])
             return carry
 
-        lax.fori_loop(0, QC, x_forward, 0)
-
-    for c in range(CHUNKS):
-        part = pl.ds(c * QC, QC)
-
-        def couple(r, carry, c=c):
+        lax.fori_loop(0, count, x_forward, 0, unroll=True)
+
+    for c, (first, count) in spans(BACKWARD):
+        part = pl.ds(first, count)
+
+        def couple(r, carry, first=first, count=count):
             rows = pl.ds(pl.multiple_of(r * 8, 8), 8)
             for lane in range(COLS // 128):
                 lanes = pl.ds(lane * 128, 128)
                 source = [spec[b, rows, lanes] for b in range(NQ)]
                 factor = {}
-                for s in range(c * QC, c * QC + QC + NQ - 1):
+                for s in range(first, first + count + NQ - 1):
                     factor[s] = gain[s, rows, lanes]
-                for a in range(QC):
+                for a in range(count):
                     total = None
                     for b in range(NQ):
-                        term = (coup[c * QC + a, b] * factor[c * QC + a + b]) * source[b]
+                        term = (coup[first + a, b] * factor[first + a + b]) * source[b]
                         total = term if total is None else total + term
                     prod[a, rows, lanes] = total
             return carry
 
         lax.fori_loop(0, NX // 8, couple, 0)
 
-        def x_inverse(a, carry, c=c):
-            send2[c * QC + a] = left_multiply(table_xi, prod[a])
+        def x_inverse(a, carry, first=first):
+            send2[first + a] = left_multiply(table_xi, prod[a])
             return carry
 
-        lax.fori_loop(0, QC, x_inverse, 0)
-
-        to_all(lambda p, row, cols, to: send(send2.at[part, p], recv2.at[part, my_row, my_cols], 4 + c, to))
-        keep(send2.at[part, me], recv2.at[part, my_row, my_cols], 4 + c)
+        lax.fori_loop(0, count, x_inverse, 0, unroll=True)
+
+        slot = FIRST_BACK + c
+        to_all(lambda p, row, cols, to: send(send2.at[part, p], recv2.at[part, my_row, my_cols], slot, to))
+        keep(send2.at[part, me], recv2.at[part, my_row, my_cols], slot)
 
     table_yi = ty_i[...]
-    for c in range(CHUNKS):
-        part = pl.ds(c * QC, QC)
-        received(recv2.at[part], 4 + c)
-        rows = right_multiply(recv2[part].reshape(QC * NY, NZ), tz, True)
-        mid[...] = rows.reshape(QC, NY, NZ)
-
-        def y_inverse(a, carry, c=c):
-            send3[c * QC + a] = left_multiply(table_yi, mid[a])
+    for c, (first, count) in spans(BACKWARD):
+        part = pl.ds(first, count)
+        received(recv2.at[part], FIRST_BACK + c)
+        rows = right_multiply(recv2[part].reshape(count * NY, NZ), tz, True)
+        mid[pl.ds(0, count)] = rows.reshape(count, NY, NZ)
+
+        def y_inverse(a, carry, first=first):
+            send3[first + a] = left_multiply(table_yi, mid[a])
             return carry
 
-        lax.fori_loop(0, QC, y_inverse, 0)
+        lax.fori_loop(0, count, y_inverse, 0, unroll=True)
 
         for dy, dz in near:
             ys = pl.ds(pl.multiple_of(gys[dy] * block_y, 8), block_y)
             zs = pl.ds(pl.multiple_of(gzs[dz] * block_z, 128), block_z)
             src, dst = send3.at[part, ys, zs], out.at[part, row_x]
             if dy or dz:
-                send(src, dst, 6 + c, {"gy": gys[dy], "gz": gzs[dz]})
+                send(src, dst, FIRST_OUT + c, {"gy": gys[dy], "gz": gzs[dz]})
             else:
-                keep(src, dst, 6 + c)
-
-    for c in range(CHUNKS):
-        received(out.at[pl.ds(c * QC, QC)], 6 + c)
+                keep(src, dst, FIRST_OUT + c)
+
+    for c, (first, count) in spans(BACKWARD):
+        received(out.at[pl.ds(first, count)], FIRST_OUT + c)
 
     sent(2 * (group - 1) * block_y * block_z // COLS, 0)
     pltpu.make_async_copy(others, others, ssem.at[1]).wait()
-    pltpu.make_async_copy(far_others, far_others, ssem.at[8]).wait()
-    for c in range(CHUNKS):
-        sent((devices - 1) * QC, 2 + c)
-        sent((devices - 1) * QC, 4 + c)
-        sent((group - 1) * QC * block_y * block_z // COLS, 6 + c)
+    pltpu.make_async_copy(far_others, far_others, ssem.at[2]).wait()
+    for c, (_, count) in spans(FORWARD):
+        sent((devices - 1) * count, FIRST_LINES + c)
+    for c, (_, count) in spans(BACKWARD):
+        sent((devices - 1) * count, FIRST_BACK + c)
+        sent((group - 1) * count * block_y * block_z // COLS, FIRST_OUT + c)
 
 
 def solution(mesh):
@@ -373,18 +400,16 @@
     bz = basis(NZ)
     tz = np.stack(halves(bz))
     by, bx = basis(NY), basis(NX)
-    fx2 = np.broadcast_to(wave_squared(NX)[:, None], (NX, 128)).astype(np.float32)
-    fz2 = np.broadcast_to(wave_squared(NZ)[None, :], (8, NZ)).astype(np.float32)
-    tables = (tz, left_table(by.T), left_table(by), left_table(bx.T), left_table(bx), fx2, fz2)
+    tables = (tz, left_table(by.T), left_table(by / Y_SCALE), left_table(bx.T), left_table(bx))
 
     def body(density, coupling):
-        vmem = pl.BlockSpec(memory_space=pltpu.VMEM)
+        vmem, anywhere = (pl.BlockSpec(memory_space=space) for space in (pltpu.VMEM, pl.ANY))
         block = density.shape
-        return pl.pallas_call(
+        fields = pl.pallas_call(
             functools.partial(kernel, sizes),
             out_shape=jax.ShapeDtypeStruct((NQ,) + block, F32),
-            in_specs=[vmem, pl.BlockSpec(memory_space=pltpu.SMEM)] + [vmem] * len(tables),
-            out_specs=vmem,
+            in_specs=[vmem, pl.BlockSpec(memory_space=pltpu.SMEM), anywhere] + [vmem] * (len(tables) - 1),
+            out_specs=anywhere,
             scratch_shapes=[
                 pltpu.VMEM((block[0] + 4, block[1] + 16, block[2]), F32),
                 pltpu.VMEM((block[2] + 16, block[0] * block[1]), F32),
@@ -396,17 +421,19 @@
                 pltpu.VMEM((sizes[1] * sizes[2], 1, 128), F32),
                 pltpu.VMEM((sizes[0], 1, 128), F32),
                 pltpu.VMEM((NQ, NY, NZ), F32),
-                pltpu.VMEM((QC, NY, NZ), F32),
+                pltpu.VMEM((max(FORWARD + BACKWARD), NY, NZ), F32),
                 pltpu.VMEM((NQ, NY, NZ), F32),
                 pltpu.VMEM((NQ, NX, COLS), F32),
                 pltpu.VMEM((NQ, NX, COLS), F32),
                 pltpu.VMEM((SUMS, NX, COLS), F32),
-                pltpu.VMEM((QC, NX, COLS), F32),
+                pltpu.VMEM((max(BACKWARD), NX, COLS), F32),
                 pltpu.VMEM((NQ, NX, COLS), F32),
                 pltpu.VMEM((NQ, NY, NZ), F32),
                 pltpu.VMEM((NQ, NY, NZ), F32),
-                pltpu.SemaphoreType.DMA((9,)),
-                pltpu.SemaphoreType.DMA((9,)),
+                pltpu.VMEM((2, NZ, NZ), BF16),
+                pltpu.SemaphoreType.DMA,
+                pltpu.SemaphoreType.DMA((SLOTS,)),
+                pltpu.SemaphoreType.DMA((SLOTS,)),
                 pltpu.SemaphoreType.DMA((8,)),
                 pltpu.SemaphoreType.DMA((8,)),
             ],
@@ -415,6 +442,7 @@
             ),
             name="convolve",
         )(density, coupling, *[jnp.asarray(t) for t in tables])
+        return fields * Y_SCALE
 
     placed = (P("gx", "gy", "gz"), P())
     return jax.shard_map(

time: 101 us -> 96.2 us (0.952)
  Pallas kernels: 98.1 us -> 93.2 us
  other arithmetic: 0 us -> 2.9 us
  local copies, waits for them, and re-layouts: 2.88 us -> 0 us
    pallas_call x1, Pallas kernels: 98.1 us -> 93.2 us  [body(): pl.pallas_call(functools.partial(kernel, sizes), out_shape=jax.ShapeDtype...]
    mul x0 -> x1, other arithmetic: none -> 2.9 us  [body(): return fields * Y_SCALE]
    unnamed x1 -> x0, local copies, waits for them, and re-layouts: 2.88 us -> none
where the time goes in v3:
time: 96.2 us; the launch traced here: 96.1 us
  Pallas kernels  93.2 us (97%)
  other arithmetic  2.9 us (3%)
    pallas_call x1, Pallas kernels, body(): pl.pallas_call(functools.partial(kernel, sizes), out_shape=jax.ShapeDtype...  93.2 us
    mul x1, other arithmetic, body(): return fields * Y_SCALE  2.9 us

profile of v3, /device:TPU:1, one launch (start us, length us, event | category | flops | bytes accessed | tf_op | source)
XLA Modules:
  0.0 96.1 jit_solution(4843124974107390419)
XLA Ops:
  0.0 93.2 %convolve.1 = f32[14,16,16,128]{3,2,1,0:T(8,128)} custom-call(f32[16,16,128]{2,1,0:T(8,128)} %dens.1, f32[14,14]{1,0:T(8,128)} %coup.1, bf16[2,512,512]{2,1,0:T(8,128)(2,1)} %constant.12.clone.tz_hbm, bf16[64,192]{1,0:T(8,128)(2,1)} %constant.13.clone.ty_f, bf16[64,192]{1,0:T(8,128)(2,1)} %constant.14.clone.ty_i, bf16[128,384]{1,0:T(8,128)(2,1)} %constant.15.clone.tx_f, ...), custom_call_target="tpu_custom_call" | custom-call | tf_op jit(solution)/shard_map/convolve/pallas_call | solution.py:408
  93.2 2.9 %broadcast_multiply_fusion = f32[14,16,16,128]{3,2,1,0:T(8,128)} fusion(f32[14,16,16,128]{3,2,1,0:T(8,128)} %convolve.1), kind=kLoop, calls=%fused_computation | loop fusion | flops 458752 | bytes 3670016 | tf_op jit(solution)/shard_map/mul | solution.py:445

commit v4 on v3

--- a/solution.py
+++ b/solution.py
@@ -29,7 +29,6 @@
 FIRST_LINES, FIRST_BACK = 3, 3 + len(FORWARD)
 FIRST_OUT = FIRST_BACK + len(BACKWARD)
 SLOTS = FIRST_OUT + len(BACKWARD)
-Y_SCALE = math.sqrt(2.0 / NY)
 
 
 def frequencies(length):
@@ -104,9 +103,9 @@
 
 
 def kernel(
-    sizes, dens, coup, tz_hbm, ty_f, ty_i, tx_f, tx_i, out,
+    sizes, dens_in, coup_in, tz_in, ty_f_in, ty_i_in, tx_f_in, tx_i_in, out,
     ext, zext, zsend, zhalo, planes, q_buf, top_src, near_tops, far_tops, thetas, mid, send1, recv1, spec, gain, prod, send2, recv2, send3,
-    tz, table_sem, ssem, rsem, hsend, hrecv,
+    dens, coup, tz, ty_f, ty_i, tx_f, tx_i, load_sem, ssem, rsem, hsend, hrecv,
 ):
     devices = NX
     nx, ny, nz = sizes
@@ -139,8 +138,11 @@
             part = recv1.at[0, 0]
             pltpu.make_async_copy(part, part, ssem.at[slot]).wait()
 
-    load_table = pltpu.make_async_copy(tz_hbm, tz, table_sem)
-    load_table.start()
+    inputs = ((dens_in, dens), (coup_in, coup), (tz_in, tz), (ty_f_in, ty_f), (ty_i_in, ty_i))
+    inputs = inputs + ((tx_f_in, tx_f), (tx_i_in, tx_i))
+    loads = [pltpu.make_async_copy(a, b, load_sem.at[k]) for k, (a, b) in enumerate(inputs)]
+    for load in loads:
+        load.start()
     z_len = nx // 2
     y_hi, z_at, y_lo, core = lax.div(ix, z_len), lax.rem(ix, z_len), lax.div(iz, 2), lax.rem(iz, 2)
     gys = [lax.rem(iy + j, ny) for j in range(ny)]
@@ -161,6 +163,7 @@
         pl.semaphore_signal(
             barrier, inc=1, device_id={"gx": gxs[dx]}, device_id_type=MESH
         )
+    loads[0].wait()
     block = dens[...]
     ext[pl.ds(2, block_x), pl.ds(8, block_y), :] = block
     turned = block.reshape(block_x * block_y, block_z).T
@@ -278,8 +281,9 @@
 
     lax.fori_loop(0, NY // 8, theta_rows, 0)
 
+    for load in loads[1:]:
+        load.wait()
     table_yf = ty_f[...]
-    load_table.wait()
     rows_of = [lax.div(g, per_row) for g in gzs]
     cols_of = [pl.ds(pl.multiple_of(lax.rem(g, per_row) * COLS, 128), COLS) for g in gzs]
 
@@ -395,21 +399,29 @@
         sent((group - 1) * count * block_y * block_z // COLS, FIRST_OUT + c)
 
 
+def write_out(fields, out, sem):
+    copies = [pltpu.make_async_copy(fields.at[a], out.at[a], sem.at[a]) for a in range(NQ)]
+    for copy in copies:
+        copy.start()
+    for copy in copies:
+        copy.wait()
+
+
 def solution(mesh):
     sizes = tuple(mesh.shape[axis] for axis in ("gx", "gy", "gz"))
     bz = basis(NZ)
     tz = np.stack(halves(bz))
     by, bx = basis(NY), basis(NX)
-    tables = (tz, left_table(by.T), left_table(by / Y_SCALE), left_table(bx.T), left_table(bx))
+    tables = (tz, left_table(by.T), left_table(by), left_table(bx.T), left_table(bx))
 
     def body(density, coupling):
-        vmem, anywhere = (pl.BlockSpec(memory_space=space) for space in (pltpu.VMEM, pl.ANY))
+        vmem, hbm = (pl.BlockSpec(memory_space=space) for space in (pltpu.VMEM, pltpu.HBM))
         block = density.shape
         fields = pl.pallas_call(
             functools.partial(kernel, sizes),
             out_shape=jax.ShapeDtypeStruct((NQ,) + block, F32),
-            in_specs=[vmem, pl.BlockSpec(memory_space=pltpu.SMEM), anywhere] + [vmem] * (len(tables) - 1),
-            out_specs=anywhere,
+            in_specs=[hbm] * (2 + len(tables)),
+            out_specs=vmem,
             scratch_shapes=[
                 pltpu.VMEM((block[0] + 4, block[1] + 16, block[2]), F32),
                 pltpu.VMEM((block[2] + 16, block[0] * block[1]), F32),
@@ -430,19 +442,30 @@
                 pltpu.VMEM((NQ, NX, COLS), F32),
                 pltpu.VMEM((NQ, NY, NZ), F32),
                 pltpu.VMEM((NQ, NY, NZ), F32),
-                pltpu.VMEM((2, NZ, NZ), BF16),
-                pltpu.SemaphoreType.DMA,
+                pltpu.VMEM(block, F32),
+                pltpu.SMEM((NQ, NQ), F32),
+                *[pltpu.VMEM(table.shape, BF16) for table in tables],
+                pltpu.SemaphoreType.DMA((2 + len(tables),)),
                 pltpu.SemaphoreType.DMA((SLOTS,)),
                 pltpu.SemaphoreType.DMA((SLOTS,)),
                 pltpu.SemaphoreType.DMA((8,)),
                 pltpu.SemaphoreType.DMA((8,)),
             ],
             compiler_params=pltpu.CompilerParams(
-                collective_id=0, has_side_effects=True, vmem_limit_bytes=56 * 1024 * 1024
+                collective_id=0, has_side_effects=True, vmem_limit_bytes=40 * 1024 * 1024
             ),
             name="convolve",
-        )(density, coupling, *[jnp.asarray(t) for t in tables])
-        return fields * Y_SCALE
+        )(*[pltpu.with_memory_space_constraint(x, pltpu.HBM) for x in (density, coupling, *map(jnp.asarray, tables))])
+        return pl.pallas_call(
+            write_out,
+            out_shape=jax.ShapeDtypeStruct((NQ,) + block, F32),
+            in_specs=[vmem],
+            out_specs=hbm,
+            scratch_shapes=[pltpu.SemaphoreType.DMA((NQ,))],
+            compiler_params=pltpu.CompilerParams(vmem_limit_bytes=4 * 1024 * 1024),
+            cost_estimate=pl.CostEstimate(flops=0, bytes_accessed=8 * NQ * density.size, transcendentals=0),
+            name="write_out",
+        )(fields)
 
     placed = (P("gx", "gy", "gz"), P())
     return jax.shard_map(

time: 96.2 us -> 93.4 us (0.971)
  other arithmetic: 2.9 us -> 0 us
    mul x1 -> x0, other arithmetic: 2.9 us -> none  [body(): return fields * Y_SCALE]
    pallas_call x0 -> x1, Pallas kernels: none -> 1.34 us  [body(): pl.pallas_call(write_out, out_shape=jax.ShapeDtypeStruct((NQ,) + block, F...]
    pallas_call x1, Pallas kernels: 93.2 us -> 92 us  [body(): pl.pallas_call(functools.partial(kernel, sizes), out_shape=jax.ShapeDtype...]
where the time goes in v4:
time: 93.4 us; the launch traced here: 93.3 us
  Pallas kernels  93.3 us (100%)
    pallas_call x1, Pallas kernels, body(): pl.pallas_call(functools.partial(kernel, sizes), out_shape=jax.ShapeDtype...  92 us

profile of v4, /device:TPU:1, one launch (start us, length us, event | category | flops | bytes accessed | tf_op | source)
XLA Modules:
  0.0 93.3 jit_solution(10390524027044248208)
XLA Ops:
  0.0 92.0 %convolve.1.fields = f32[14,16,16,128]{3,2,1,0:T(8,128)S(1)} custom-call(f32[16,16,128]{2,1,0:T(8,128)} %dens_in.1, f32[14,14]{1,0:T(8,128)} %coup_in.1, bf16[2,512,512]{2,1,0:T(8,128)(2,1)} %constant.10.clone.tz_in, bf16[64,192]{1,0:T(8,128)(2,1)} %constant.11.clone.ty_f_in, bf16[64,192]{1,0:T(8,128)(2,1)} %constant.12.clone.ty_i_in, ...), custom_call_target="tpu_custom_call" | custom-call | tf_op jit(solution)/shard_map/convolve/pallas_call | solution.py:420
  92.0 1.3 %write_out.1 = f32[14,16,16,128]{3,2,1,0:T(8,128)} custom-call(f32[14,16,16,128]{3,2,1,0:T(8,128)S(1)} %convolve.1.fields), custom_call_target="tpu_custom_call" | custom-call | bytes 3670016 | tf_op jit(solution)/shard_map/write_out/pallas_call | solution.py:459

commit v5 on v4

--- a/solution.py
+++ b/solution.py
@@ -16,7 +16,8 @@
 NQ = 14
 NX, NY, NZ = 128, 64, 512
 FORWARD = (5, 9)
-BACKWARD = (4, 5, 5)
+BACKWARD = (4, 3, 3, 4)
+ROUTES = "QPQP"
 KNOTS = NQ + 2
 COLS = NY * NZ // NX
 SUMS = 2 * NQ - 1
@@ -27,8 +28,7 @@
 LOCAL = 0.25
 LAM = math.sqrt(3.0) - 2.0
 FIRST_LINES, FIRST_BACK = 3, 3 + len(FORWARD)
-FIRST_OUT = FIRST_BACK + len(BACKWARD)
-SLOTS = FIRST_OUT + len(BACKWARD)
+SLOTS = FIRST_BACK + 3 * len(BACKWARD)
 
 
 def frequencies(length):
@@ -65,6 +65,7 @@
 
 
 ORDER = far_first()
+LINE_ORDER = [(dx, dz) for dx, dy, dz in ORDER if dy == 0] + [(0, 0)]
 
 
 def halves(table):
@@ -104,7 +105,7 @@
 
 def kernel(
     sizes, dens_in, coup_in, tz_in, ty_f_in, ty_i_in, tx_f_in, tx_i_in, out,
-    ext, zext, zsend, zhalo, planes, q_buf, top_src, near_tops, far_tops, thetas, mid, send1, recv1, spec, gain, prod, send2, recv2, send3,
+    ext, zext, zsend, zhalo, planes, q_buf, top_src, near_tops, far_tops, thetas, mid, send1, recv1, spec, gain, prod, send2, y_in, y_out, z_in_p, z_in_q, z_out_p, z_out_q,
     dens, coup, tz, ty_f, ty_i, tx_f, tx_i, load_sem, ssem, rsem, hsend, hrecv,
 ):
     devices = NX
@@ -113,7 +114,6 @@
     ix, iy, iz = lax.axis_index("gx"), lax.axis_index("gy"), lax.axis_index("gz")
     me = (ix * ny + iy) * nz + iz
     block_x, block_y, block_z = NX // nx, NY // ny, NZ // nz
-    per_row = NZ // COLS
 
     def send(src, dst, slot, to):
         pltpu.make_async_remote_copy(
@@ -129,13 +129,13 @@
     def sent(rows, slot):
         full, rest = divmod(rows, NX)
         if full:
-            part = recv1.at[pl.ds(0, full)]
+            part = spec.at[pl.ds(0, full)]
             pltpu.make_async_copy(part, part, ssem.at[slot]).wait()
         if rest // 8:
-            part = recv1.at[0, pl.ds(0, rest // 8 * 8)]
+            part = spec.at[0, pl.ds(0, rest // 8 * 8)]
             pltpu.make_async_copy(part, part, ssem.at[slot]).wait()
         for _ in range(rest % 8):
-            part = recv1.at[0, 0]
+            part = spec.at[0, 0]
             pltpu.make_async_copy(part, part, ssem.at[slot]).wait()
 
     inputs = ((dens_in, dens), (coup_in, coup), (tz_in, tz), (ty_f_in, ty_f), (ty_i_in, ty_i))
@@ -284,16 +284,10 @@
     for load in loads[1:]:
         load.wait()
     table_yf = ty_f[...]
-    rows_of = [lax.div(g, per_row) for g in gzs]
-    cols_of = [pl.ds(pl.multiple_of(lax.rem(g, per_row) * COLS, 128), COLS) for g in gzs]
-
-    def to_all(issue):
-        for dx, dy, dz in ORDER:
-            p = (gxs[dx] * ny + gys[dy]) * nz + gzs[dz]
-            row = (gxs[dx] * ny + gys[dy]) * (nz // per_row) + rows_of[dz]
-            issue(p, row, cols_of[dz], {"gx": gxs[dx], "gy": gys[dy], "gz": gzs[dz]})
-
-    my_row, my_cols = lax.div(me, per_row), pl.ds(pl.multiple_of(lax.rem(me, per_row) * COLS, 128), COLS)
+    quarter = [pl.ds(pl.multiple_of(g * 128, 128), 128) for g in gys]
+    z_part = [pl.ds(pl.multiple_of(g * block_z, 128), block_z) for g in gzs]
+    my_line = ix * nz + iz
+
     for c, (first, count) in spans(FORWARD):
         part = pl.ds(first, count)
 
@@ -303,14 +297,19 @@
 
         lax.fori_loop(0, count, y_forward, 0, unroll=True)
         rows = right_multiply(mid[pl.ds(0, count)].reshape(count * NY, NZ), tz, False)
-        send1[part] = rows.reshape(count, NY, NZ)
+        send1[part] = rows.reshape(count, 2, NY // 2, NZ)
 
         slot = FIRST_LINES + c
-        to_all(lambda p, row, cols, to: send(send1.at[part, row, cols], recv1.at[part, me], slot, to))
-        keep(send1.at[part, my_row, my_cols], recv1.at[part, me], slot)
-
-    col = lax.broadcasted_iota(jnp.int32, (8, COLS), 1) + lax.rem(me, per_row) * COLS
-    yz2 = wave_squared(my_row, NY) + wave_squared(col, NZ)
+        for dx, dy, dz in ORDER:
+            src = send1.at[part, :, gxs[dx] * nz + gzs[dz], quarter[dy]]
+            to = {"gx": gxs[dx], "gy": gys[dy], "gz": gzs[dz]}
+            send(src, recv1.at[part, :, me, :], slot, to)
+        keep(send1.at[part, :, my_line, quarter[0]], recv1.at[part, :, me, :], slot)
+
+    col = lax.broadcasted_iota(jnp.int32, (8, COLS), 1)
+    wave_y = jnp.where(col < 128, my_line, my_line + NY // 2)
+    wave_z = jnp.where(col < 128, col, col - 128) + iy * 128
+    yz2 = wave_squared(wave_y, NY) + wave_squared(wave_z, NZ)
     top_sq = jnp.broadcast_to(q_top * q_top, (8, COLS))
 
     def gain_rows(r, carry):
@@ -324,11 +323,27 @@
     lax.fori_loop(0, NX // 8, gain_rows, 0)
 
     table_xf, table_xi = tx_f[...], tx_i[...]
+
+    def over_y(src, dst, dy, slot):
+        if dy:
+            send(src, dst, slot, {"gy": gys[dy]})
+        else:
+            keep(src, dst, slot)
+
+    def over_line(src, part, dx, dz, slot):
+        dst = y_in.at[part, :, :, my_line, :]
+        if dx or dz:
+            send(src, dst, slot, {"gx": gxs[dx], "gz": gzs[dz]})
+        else:
+            keep(src, dst, slot)
+
     for c, (first, count) in spans(FORWARD):
         received(recv1.at[pl.ds(first, count)], FIRST_LINES + c)
 
         def x_forward(a, carry, first=first):
-            spec[first + a] = left_multiply(table_xf, recv1[first + a])
+            lines = recv1[first + a]
+            lines = jnp.concatenate([lines[0], lines[1]], axis=1)
+            spec[first + a] = left_multiply(table_xf, lines)
             return carry
 
         lax.fori_loop(0, count, x_forward, 0, unroll=True)
@@ -355,39 +370,78 @@
         lax.fori_loop(0, NX // 8, couple, 0)
 
         def x_inverse(a, carry, first=first):
-            send2[first + a] = left_multiply(table_xi, prod[a])
+            lines = left_multiply(table_xi, prod[a])
+            for r in range(2):
+                send2[first + a, r] = lines[:, 128 * r : 128 * r + 128].reshape(4, NX // 4, 128)
             return carry
 
         lax.fori_loop(0, count, x_inverse, 0, unroll=True)
 
-        slot = FIRST_BACK + c
-        to_all(lambda p, row, cols, to: send(send2.at[part, p], recv2.at[part, my_row, my_cols], slot, to))
-        keep(send2.at[part, me], recv2.at[part, my_row, my_cols], slot)
+        slot = FIRST_BACK + 3 * c
+        if ROUTES[c] == "P":
+            for dx, dz in LINE_ORDER:
+                src = send2.at[part, :, :, gzs[dz] * nx + gxs[dx], :]
+                over_line(src, part, dx, dz, slot)
+        else:
+            for dy in (2, 1, 3, 0):
+                src, dst = send2.at[part, :, gys[dy]], z_in_q.at[part, :, :, quarter[0]]
+                over_y(src, dst, dy, slot)
 
     table_yi = ty_i[...]
+
+    def y_inverse_all(first, count):
+        def y_inverse(a, carry):
+            planes_of = [
+                jnp.concatenate([y_in[first + a, 0, k], y_in[first + a, 1, k]], axis=0)
+                for k in range(4)
+            ]
+            rows = left_multiply(table_yi, jnp.concatenate(planes_of, axis=1))
+            for k in range(4):
+                y_out[first + a, k] = rows[:, 128 * k : 128 * k + 128]
+            return carry
+
+        lax.fori_loop(0, count, y_inverse, 0, unroll=True)
+
+    def rows_for(dy):
+        return pl.ds(pl.multiple_of(gys[dy] * block_y, 8), block_y)
+
     for c, (first, count) in spans(BACKWARD):
         part = pl.ds(first, count)
-        received(recv2.at[part], FIRST_BACK + c)
-        rows = right_multiply(recv2[part].reshape(count * NY, NZ), tz, True)
-        mid[pl.ds(0, count)] = rows.reshape(count, NY, NZ)
-
-        def y_inverse(a, carry, first=first):
-            send3[first + a] = left_multiply(table_yi, mid[a])
-            return carry
-
-        lax.fori_loop(0, count, y_inverse, 0, unroll=True)
-
-        for dy, dz in near:
-            ys = pl.ds(pl.multiple_of(gys[dy] * block_y, 8), block_y)
-            zs = pl.ds(pl.multiple_of(gzs[dz] * block_z, 128), block_z)
-            src, dst = send3.at[part, ys, zs], out.at[part, row_x]
-            if dy or dz:
-                send(src, dst, FIRST_OUT + c, {"gy": gys[dy], "gz": gzs[dz]})
-            else:
-                keep(src, dst, FIRST_OUT + c)
+        slot = FIRST_BACK + 3 * c
+        received((y_in if ROUTES[c] == "P" else z_in_q).at[part], slot)
+        if ROUTES[c] == "P":
+            y_inverse_all(first, count)
+            for dy in (2, 1, 3, 0):
+                src, dst = y_out.at[part, :, rows_for(dy), :], z_in_p.at[part, :, :, quarter[0]]
+                over_y(src, dst, dy, slot + 1)
+        else:
+            rows = right_multiply(z_in_q[part].reshape(count * NY, NZ), tz, True)
+            z_out_q[part] = rows.reshape(count, 2, 4, nx, NZ)
+            for dx, dz in LINE_ORDER:
+                z_of = z_part[dz]
+                src = z_out_q.at[part, :, :, gxs[dx], z_of]
+                over_line(src, part, dx, dz, slot + 1)
 
     for c, (first, count) in spans(BACKWARD):
-        received(out.at[pl.ds(first, count)], FIRST_OUT + c)
+        part = pl.ds(first, count)
+        slot = FIRST_BACK + 3 * c
+        received((z_in_p if ROUTES[c] == "P" else y_in).at[part], slot + 1)
+        if ROUTES[c] == "P":
+            rows = right_multiply(z_in_p[part].reshape(count * NY, NZ), tz, True)
+            z_out_p[part] = rows.reshape(count, 4, block_y, NZ)
+            for dz in (2, 3, 1, 0):
+                src, dst = z_out_p.at[part, :, :, z_part[dz]], out.at[part, :, iz]
+                if dz:
+                    send(src, dst, slot + 2, {"gz": gzs[dz]})
+                else:
+                    keep(src, dst, slot + 2)
+        else:
+            y_inverse_all(first, count)
+            for dy in (2, 1, 3, 0):
+                over_y(y_out.at[part, :, rows_for(dy), :], out.at[part, iy], dy, slot + 2)
+
+    for c, (first, count) in spans(BACKWARD):
+        received(out.at[pl.ds(first, count)], FIRST_BACK + 3 * c + 2)
 
     sent(2 * (group - 1) * block_y * block_z // COLS, 0)
     pltpu.make_async_copy(others, others, ssem.at[1]).wait()
@@ -395,8 +449,9 @@
     for c, (_, count) in spans(FORWARD):
         sent((devices - 1) * count, FIRST_LINES + c)
     for c, (_, count) in spans(BACKWARD):
-        sent((devices - 1) * count, FIRST_BACK + c)
-        sent((group - 1) * count * block_y * block_z // COLS, FIRST_OUT + c)
+        few, many = 3 * 32 * count, (nx * nz - 1) * 4 * count
+        for k, rows in enumerate((many, few, few) if ROUTES[c] == "P" else (few, many, few)):
+            sent(rows, FIRST_BACK + 3 * c + k)
 
 
 def write_out(fields, out, sem):
@@ -412,14 +467,15 @@
     bz = basis(NZ)
     tz = np.stack(halves(bz))
     by, bx = basis(NY), basis(NX)
-    tables = (tz, left_table(by.T), left_table(by), left_table(bx.T), left_table(bx))
+    x_rows = np.arange(NX).reshape(8, 4, 4).transpose(1, 2, 0).reshape(-1)
+    tables = (tz, left_table(by.T), left_table(by), left_table(bx.T), left_table(bx[x_rows]))
 
     def body(density, coupling):
         vmem, hbm = (pl.BlockSpec(memory_space=space) for space in (pltpu.VMEM, pltpu.HBM))
         block = density.shape
         fields = pl.pallas_call(
             functools.partial(kernel, sizes),
-            out_shape=jax.ShapeDtypeStruct((NQ,) + block, F32),
+            out_shape=jax.ShapeDtypeStruct((NQ, 4, block[0] // 4) + block[1:], F32),
             in_specs=[hbm] * (2 + len(tables)),
             out_specs=vmem,
             scratch_shapes=[
@@ -433,15 +489,19 @@
                 pltpu.VMEM((sizes[1] * sizes[2], 1, 128), F32),
                 pltpu.VMEM((sizes[0], 1, 128), F32),
                 pltpu.VMEM((NQ, NY, NZ), F32),
-                pltpu.VMEM((max(FORWARD + BACKWARD), NY, NZ), F32),
-                pltpu.VMEM((NQ, NY, NZ), F32),
-                pltpu.VMEM((NQ, NX, COLS), F32),
+                pltpu.VMEM((max(FORWARD), NY, NZ), F32),
+                pltpu.VMEM((NQ, 2, NY // 2, NZ), F32),
+                pltpu.VMEM((NQ, 2, NX, 128), F32),
                 pltpu.VMEM((NQ, NX, COLS), F32),
                 pltpu.VMEM((SUMS, NX, COLS), F32),
                 pltpu.VMEM((max(BACKWARD), NX, COLS), F32),
-                pltpu.VMEM((NQ, NX, COLS), F32),
-                pltpu.VMEM((NQ, NY, NZ), F32),
-                pltpu.VMEM((NQ, NY, NZ), F32),
+                pltpu.VMEM((NQ, 2, 4, NX // 4, 128), F32),
+                pltpu.VMEM((NQ, 2, 4, NY // 2, 128), F32),
+                pltpu.VMEM((NQ, 4, NY, 128), F32),
+                pltpu.VMEM((NQ, 4, NY // 4, NZ), F32),
+                pltpu.VMEM((NQ, 2, NX // 4, NZ), F32),
+                pltpu.VMEM((NQ, 4, NY // 4, NZ), F32),
+                pltpu.VMEM((NQ, 2, 4, NX // 16, NZ), F32),
                 pltpu.VMEM(block, F32),
                 pltpu.SMEM((NQ, NQ), F32),
                 *[pltpu.VMEM(table.shape, BF16) for table in tables],
@@ -465,7 +525,7 @@
             compiler_params=pltpu.CompilerParams(vmem_limit_bytes=4 * 1024 * 1024),
             cost_estimate=pl.CostEstimate(flops=0, bytes_accessed=8 * NQ * density.size, transcendentals=0),
             name="write_out",
-        )(fields)
+        )(fields.reshape((NQ,) + block))
 
     placed = (P("gx", "gy", "gz"), P())
     return jax.shard_map(

time: 93.4 us -> 84.1 us (0.900)
  Pallas kernels: 93.3 us -> 83.9 us
    pallas_call x1, Pallas kernels: 92 us -> 82.6 us  [body(): pl.pallas_call(functools.partial(kernel, sizes), out_shape=jax.ShapeDtype...]
where the time goes in v5:
time: 84.1 us; the launch traced here: 84 us
  Pallas kernels  83.9 us (100%)
    pallas_call x1, Pallas kernels, body(): pl.pallas_call(functools.partial(kernel, sizes), out_shape=jax.ShapeDtype...  82.6 us

profile of v5, /device:TPU:1, one launch (start us, length us, event | category | flops | bytes accessed | tf_op | source)
XLA Modules:
  0.0 84.0 jit_solution(2379853628580229575)
XLA Ops:
  0.0 82.6 %convolve.1 = f32[14,4,4,16,128]{4,3,2,1,0:T(8,128)S(1)} custom-call(f32[16,16,128]{2,1,0:T(8,128)} %dens_in.1, f32[14,14]{1,0:T(8,128)} %coup_in.1, bf16[2,512,512]{2,1,0:T(8,128)(2,1)} %constant.10.clone.tz_in, bf16[64,192]{1,0:T(8,128)(2,1)} %constant.11.clone.ty_f_in, bf16[64,192]{1,0:T(8,128)(2,1)} %constant.12.clone.ty_i_in, ...), custom_call_target="tpu_custom_call" | custom-call | tf_op jit(solution)/shard_map/convolve/pallas_call | solution.py:476
  82.6 1.3 %write_out.1 = f32[14,16,16,128]{3,2,1,0:T(8,128)} custom-call(f32[14,16,16,128]{3,2,1,0:T(8,128)S(1)} %bitcast.1), custom_call_target="tpu_custom_call" | custom-call | bytes 3670016 | tf_op jit(solution)/shard_map/write_out/pallas_call | solution.py:519

commit v6 on v5

--- a/solution.py
+++ b/solution.py
@@ -15,9 +15,10 @@
 
 NQ = 14
 NX, NY, NZ = 128, 64, 512
-FORWARD = (5, 9)
-BACKWARD = (4, 3, 3, 4)
-ROUTES = "QPQP"
+FORWARD = (3, 5, 6)
+BACKWARD = (2, 3, 3, 3, 3)
+ROUTES = "PQPQP"
+LAG = 5
 KNOTS = NQ + 2
 COLS = NY * NZ // NX
 SUMS = 2 * NQ - 1
@@ -405,7 +406,7 @@
     def rows_for(dy):
         return pl.ds(pl.multiple_of(gys[dy] * block_y, 8), block_y)
 
-    for c, (first, count) in spans(BACKWARD):
+    def middle(c, first, count):
         part = pl.ds(first, count)
         slot = FIRST_BACK + 3 * c
         received((y_in if ROUTES[c] == "P" else z_in_q).at[part], slot)
@@ -422,7 +423,7 @@
                 src = z_out_q.at[part, :, :, gxs[dx], z_of]
                 over_line(src, part, dx, dz, slot + 1)
 
-    for c, (first, count) in spans(BACKWARD):
+    def last(c, first, count):
         part = pl.ds(first, count)
         slot = FIRST_BACK + 3 * c
         received((z_in_p if ROUTES[c] == "P" else y_in).at[part], slot + 1)
@@ -439,6 +440,15 @@
             y_inverse_all(first, count)
             for dy in (2, 1, 3, 0):
                 over_y(y_out.at[part, :, rows_for(dy), :], out.at[part, iy], dy, slot + 2)
+
+    chunks = spans(BACKWARD)
+    for k in range(len(chunks) + LAG):
+        if k < len(chunks):
+            c, (first, count) = chunks[k]
+            middle(c, first, count)
+        if k >= LAG:
+            c, (first, count) = chunks[k - LAG]
+            last(c, first, count)
 
     for c, (first, count) in spans(BACKWARD):
         received(out.at[pl.ds(first, count)], FIRST_BACK + 3 * c + 2)

time: 84.1 us -> 81.9 us (0.974)
  Pallas kernels: 83.9 us -> 81.7 us
    pallas_call x1, Pallas kernels: 82.6 us -> 80.4 us  [body(): pl.pallas_call(functools.partial(kernel, sizes), out_shape=jax.ShapeDtype...]
where the time goes in v6:
time: 81.9 us; the launch traced here: 81.8 us
  Pallas kernels  81.7 us (100%)
    pallas_call x1, Pallas kernels, body(): pl.pallas_call(functools.partial(kernel, sizes), out_shape=jax.ShapeDtype...  80.4 us

profile of v6, /device:TPU:1, one launch (start us, length us, event | category | flops | bytes accessed | tf_op | source)
XLA Modules:
  0.0 81.8 jit_solution(8130949061730200588)
XLA Ops:
  0.0 80.4 %convolve.1 = f32[14,4,4,16,128]{4,3,2,1,0:T(8,128)S(1)} custom-call(f32[16,16,128]{2,1,0:T(8,128)} %dens_in.1, f32[14,14]{1,0:T(8,128)} %coup_in.1, bf16[2,512,512]{2,1,0:T(8,128)(2,1)} %constant.10.clone.tz_in, bf16[64,192]{1,0:T(8,128)(2,1)} %constant.11.clone.ty_f_in, bf16[64,192]{1,0:T(8,128)(2,1)} %constant.12.clone.ty_i_in, ...), custom_call_target="tpu_custom_call" | custom-call | tf_op jit(solution)/shard_map/convolve/pallas_call | solution.py:486
  80.4 1.3 %write_out.1 = f32[14,16,16,128]{3,2,1,0:T(8,128)} custom-call(f32[14,16,16,128]{3,2,1,0:T(8,128)S(1)} %bitcast.1), custom_call_target="tpu_custom_call" | custom-call | bytes 3670016 | tf_op jit(solution)/shard_map/write_out/pallas_call | solution.py:529

commit v7 on v6

--- a/solution.py
+++ b/solution.py
@@ -106,7 +106,7 @@
 
 def kernel(
     sizes, dens_in, coup_in, tz_in, ty_f_in, ty_i_in, tx_f_in, tx_i_in, out,
-    ext, zext, zsend, zhalo, planes, q_buf, top_src, near_tops, far_tops, thetas, mid, send1, recv1, spec, gain, prod, send2, y_in, y_out, z_in_p, z_in_q, z_out_p, z_out_q,
+    ext, zext, zsend, zhalo, planes, q_buf, top_src, near_tops, far_tops, thetas, mid, send1, recv1, spec, gain, link, prod, send2, y_in, y_out, z_in_p, z_in_q, z_out_p, z_out_q,
     dens, coup, tz, ty_f, ty_i, tx_f, tx_i, load_sem, ssem, rsem, hsend, hrecv,
 ):
     devices = NX
@@ -250,10 +250,10 @@
         send(top_src.at[1], far_tops.at[ix], 2, {"gx": gxs[dx]})
     far_others = far_tops.at[pl.ds(0, nx - 1)]
     received(far_others, 2)
-    q_top = jnp.max(far_tops[...])
+    q_top = jnp.broadcast_to(jnp.max(far_tops[...], axis=0), (8, 128))
     received(planes, 0)
 
-    inv_top = 1.0 / jnp.broadcast_to(q_top, (8, 128))
+    inv_top = 1.0 / q_top
     weight = math.sqrt(3.0) / 6.0
 
     def theta_rows(r, carry):
@@ -311,14 +311,18 @@
     wave_y = jnp.where(col < 128, my_line, my_line + NY // 2)
     wave_z = jnp.where(col < 128, col, col - 128) + iy * 128
     yz2 = wave_squared(wave_y, NY) + wave_squared(wave_z, NZ)
-    top_sq = jnp.broadcast_to(q_top * q_top, (8, COLS))
+    top_sq = jnp.concatenate([q_top * q_top] * (COLS // 128), axis=1)
 
     def gain_rows(r, carry):
         rows = pl.ds(pl.multiple_of(r * 8, 8), 8)
         k_sq = wave_squared(lax.broadcasted_iota(jnp.int32, (8, COLS), 0) + r * 8, NX) + yz2
         for s in range(SUMS):
             mass = top_sq * math.exp(-STEP * (2 * NQ - 2 - s))
-            gain[s, rows, :] = LOCAL + mass / (k_sq + mass)
+            value = LOCAL + mass / (k_sq + mass)
+            gain[s, rows, :] = value
+            for a in range(BACKWARD[0]):
+                if 0 <= s - a < NQ:
+                    link[a, s - a, rows, :] = coup[a, s - a] * value
         return carry
 
     lax.fori_loop(0, NX // 8, gain_rows, 0)
@@ -359,11 +363,16 @@
                 source = [spec[b, rows, lanes] for b in range(NQ)]
                 factor = {}
                 for s in range(first, first + count + NQ - 1):
-                    factor[s] = gain[s, rows, lanes]
+                    if first:
+                        factor[s] = gain[s, rows, lanes]
                 for a in range(count):
                     total = None
                     for b in range(NQ):
-                        term = (coup[first + a, b] * factor[first + a + b]) * source[b]
+                        if first:
+                            weight = coup[first + a, b] * factor[first + a + b]
+                        else:
+                            weight = link[a, b, rows, lanes]
+                        term = weight * source[b]
                         total = term if total is None else total + term
                     prod[a, rows, lanes] = total
             return carry
@@ -504,6 +513,7 @@
                 pltpu.VMEM((NQ, 2, NX, 128), F32),
                 pltpu.VMEM((NQ, NX, COLS), F32),
                 pltpu.VMEM((SUMS, NX, COLS), F32),
+                pltpu.VMEM((BACKWARD[0], NQ, NX, COLS), F32),
                 pltpu.VMEM((max(BACKWARD), NX, COLS), F32),
                 pltpu.VMEM((NQ, 2, 4, NX // 4, 128), F32),
                 pltpu.VMEM((NQ, 2, 4, NY // 2, 128), F32),

time: 81.9 us -> 81.7 us (level)
  no operation moved by 1% of the time
where the time goes in v7:
time: 81.7 us; the launch traced here: 81.6 us
  Pallas kernels  81.6 us (100%)
    pallas_call x1, Pallas kernels, body(): pl.pallas_call(functools.partial(kernel, sizes), out_shape=jax.ShapeDtype...  80.2 us

profile of v7, /device:TPU:1, one launch (start us, length us, event | category | flops | bytes accessed | tf_op | source)
XLA Modules:
  0.0 81.6 jit_solution(8607008254698887099)
XLA Ops:
  0.0 80.2 %convolve.1 = f32[14,4,4,16,128]{4,3,2,1,0:T(8,128)S(1)} custom-call(f32[16,16,128]{2,1,0:T(8,128)} %dens_in.1, f32[14,14]{1,0:T(8,128)} %coup_in.1, bf16[2,512,512]{2,1,0:T(8,128)(2,1)} %constant.10.clone.tz_in, bf16[64,192]{1,0:T(8,128)(2,1)} %constant.11.clone.ty_f_in, bf16[64,192]{1,0:T(8,128)(2,1)} %constant.12.clone.ty_i_in, ...), custom_call_target="tpu_custom_call" | custom-call | tf_op jit(solution)/shard_map/convolve/pallas_call | solution.py:495
  80.2 1.3 %write_out.1 = f32[14,16,16,128]{3,2,1,0:T(8,128)} custom-call(f32[14,16,16,128]{3,2,1,0:T(8,128)S(1)} %bitcast.1), custom_call_target="tpu_custom_call" | custom-call | bytes 3670016 | tf_op jit(solution)/shard_map/write_out/pallas_call | solution.py:539
